TPU v7x, 32 devices: a whole 2x2x4 slice. The times are simulated.
32 devices in a mesh: groups: 2 (over x), seq: 8 (over z, y), section: 2 (over core).
Axes of the slice: x: 2, y: 2, z: 4, core: 2. Of those that a mesh axis runs over, the one named last changes fastest.
Arguments:
- latent_cache: bfloat16 [2, 8, 32768, 576], P('section', 'groups', 'seq'), parts along dimension 1, may hold values from -6 to 6
- index_keys: bfloat16 [2, 8, 32768, 128], P('section', 'groups', 'seq'), parts along dimension 1, may hold values from -6 to 6
- latent_query: bfloat16 [2, 8, 128, 576], P('section', 'groups', 'seq'), parts along dimension 1, may hold values from -54 to 54
- index_query: bfloat16 [2, 8, 64, 128], P('section', 'groups', 'seq'), parts along dimension 1, may hold values from -6 to 6
- index_weight: bfloat16 [2, 8, 64], P('section', 'groups', 'seq'), parts along dimension 1, may hold values from -0.75 to 0.75
- value_up_weight: bfloat16 [2, 128, 512, 128], P('section', 'seq'), may hold values from -0.25 to 0.25
- selected: int32 [2, 8, 2, 32], P('section', 'groups'), parts along dimension 1, may hold values from 0 to 511, as said below
- lengths: int32 [8], P('groups'), parts along dimension 0, may hold values from 16384 to 32767, as said below
Outputs:
- index_scores: float32 [2, 8, 32768], P('section', 'groups', 'seq'), parts along dimension 1
- head_out: bfloat16 [2, 8, 128, 128], P('section', 'groups', 'seq'), parts along dimension 1
There are 2 independent parts, one for each index of `groups`. A program takes and returns all parts, laid end to end along the dimension named above; an argument that names none is the same for every part. Nothing has to cross between parts.
Inputs may be any that keep to these rules, and one draw needn't show every extreme that they name: `lengths`: never one more than a multiple of 64. `selected`: for each layer, row and head group, 32 distinct block numbers, each block starting before the row's length; the block holding the row's last live token is always among them.
All inputs are finite; a program needn't handle non-finite values.
Results may differ from a plain program's by a relative error of at most 0.0048.
Values may be sent and summed in bfloat16 or wider, within the bound.
A program may use at most 128 MiB of HBM per device.

v0:
```python
import jax
import jax.numpy as jnp
from jax import lax
from jax.sharding import PartitionSpec as P

LATENT_WIDTH = 512
ROTARY_WIDTH = 64
VALUE_WIDTH = 128
IDX_DIM = 128
BLOCK = 64
HEAD_GROUPS = 2


def finish(total_per_row, partial_output, projection):
    attended = (partial_output / total_per_row[..., None]).astype(jnp.bfloat16)
    return jnp.einsum(
        "bhc,hcv->bhv", attended, projection, preferred_element_type=jnp.float32
    ).astype(jnp.bfloat16)


def on_device(
    latent_cache,
    index_keys,
    latent_query,
    index_query,
    index_weight,
    value_up_weight,
    selected,
    lengths,
):
    latent_state = latent_cache[0]
    index_rows = index_keys[0]
    projection = value_up_weight[0]
    chosen = selected[0]
    seq_index = lax.axis_index("seq")
    span = latent_state.shape[1]
    gathered = (
        lax.all_gather(latent_query, "seq", axis=2, tiled=True),
        lax.all_gather(index_query, "seq", axis=2, tiled=True),
        lax.all_gather(index_weight, "seq", axis=2, tiled=True),
    )
    queries = gathered[0][0]
    index_heads = gathered[1][0]
    head_weights = gathered[2][0].astype(jnp.float32)
    positions = seq_index * span + jnp.arange(span, dtype=jnp.int32)
    live_mask = positions[None, :] < lengths[:, None]
    index_dots = jnp.einsum(
        "bhd,btd->bht", index_heads, index_rows, preferred_element_type=jnp.float32
    )
    weighted = jax.nn.relu(index_dots * IDX_DIM ** (-0.5)) * head_weights[:, :, None]
    index_scores = jnp.where(live_mask, jnp.sum(weighted, axis=1), jnp.float32(0.0))
    block_ids = positions // BLOCK
    hit_mask = jnp.any(chosen[:, :, :, None] == block_ids[None, None, None, :], axis=2)
    usable = (hit_mask & live_mask[:, None, :])[:, :, None, :]
    count_of_rows = queries.shape[0]
    every_head = queries.shape[1]
    group_wise = every_head // HEAD_GROUPS
    group_split = queries.reshape(count_of_rows, HEAD_GROUPS, group_wise, queries.shape[2])
    scores = jnp.einsum(
        "bghd,btd->bght", group_split, latent_state, preferred_element_type=jnp.float32
    ) * (VALUE_WIDTH + ROTARY_WIDTH) ** (-0.5)
    masked = jnp.where(usable, scores, jnp.float32(-1e30))
    row_max = jnp.max(masked, axis=3)
    soft_weights = jnp.where(usable, jnp.exp(masked - row_max[..., None]), jnp.float32(0.0))
    total_per_row = jnp.sum(soft_weights, axis=3)
    partial_output = jnp.einsum(
        "bght,btv->bghv",
        soft_weights.astype(jnp.bfloat16),
        latent_state[:, :, :LATENT_WIDTH],
        preferred_element_type=jnp.float32,
    )
    row_max = row_max.reshape(count_of_rows, every_head)
    total_per_row = total_per_row.reshape(count_of_rows, every_head)
    partial_output = partial_output.reshape(count_of_rows, every_head, LATENT_WIDTH)
    source_max = lax.all_to_all(row_max[None], "seq", split_axis=2, concat_axis=0, tiled=True)
    source_total = lax.all_to_all(
        total_per_row[None], "seq", split_axis=2, concat_axis=0, tiled=True
    )
    source_out = lax.all_to_all(
        partial_output[None], "seq", split_axis=2, concat_axis=0, tiled=True
    )
    joint_max = jnp.max(source_max, axis=0)
    factor = jnp.exp(source_max - joint_max[None])
    joint_total = jnp.sum(source_total * factor, axis=0)
    joint_out = jnp.sum(source_out * factor[..., None], axis=0)
    head_out = finish(joint_total, joint_out, projection)
    return (index_scores[None], head_out[None])


def solution(mesh):
    return jax.shard_map(
        on_device,
        mesh=mesh,
        in_specs=(
            P("section", "groups", "seq", None),
            P("section", "groups", "seq", None),
            P("section", "groups", "seq", None),
            P("section", "groups", "seq", None),
            P("section", "groups", "seq"),
            P("section", "seq", None, None),
            P("section", "groups", None, None),
            P("groups"),
        ),
        out_specs=(P("section", "groups", "seq"), P("section", "groups", "seq", None)),
        check_vma=False,
    )
```

profile of v0, /device:TPU:0, one launch (start us, length us, event | category | flops | bytes accessed | tf_op | source)
XLA Modules:
  0.0 179.4 jit_solution(9175186861253746347)
XLA Ops:
  0.7 33.8 %all_gather.11 = bf16[1,4,128,576]{3,2,1,0:T(8,128)(2,1)S(1)} all-gather(bf16[1,4,16,576]{3,2,1,0:T(8,128)(2,1)} %param.10), channel_id=1, replica_groups=mesh['groups'=2,'seq'=8,'section'=2] {'seq'}, dimensions={2}, use_global_device_ids=true | all-gather | bytes 663552 | tf_op jit(solution)/shard_map/all_gather | solution.py:38
  34.4 0.7 broadcast_compare_fusion
  35.2 1.6 compare_reduce_fusion
  36.8 0.1 broadcast_and_fusion
  36.9 8.7 %fusion.3 = (f32[4,2,64]{2,1,0:T(2,128)S(1)}, f32[4,2,64,4096]{3,2,1,0:T(8,128)S(1)}) fusion(pred[4,2,4096]{2,1,0:T(4,128)(4,1)S(1)} %broadcast_and_fusion, bf16[4,2,64,576]{3,2,1,0:T(8,128)(2,1)S(1)} %bitcast.68, bf16[1,4,4096,576]{2,3,1,0:T(8,128)(2,1)} %param.8), kind=kOutput, calls=%fused_computation.6 | convolution fusion | flops 2422210048 | bytes 27887616 | tf_op jit(solution)/shard_map/bghd,btd->bght/dot_general | solution.py:59
  45.7 3.3 %copy-done.1 = f32[4,2,64,4096]{3,2,1,0:T(8,128)} copy-done((f32[4,2,64,4096]{3,2,1,0:T(8,128)}, f32[4,2,64,4096]{3,2,1,0:T(8,128)S(1)}, u32[]{:S(2)}) %copy-start.1) | copy-done | bytes 8388632
  48.9 2.9 %fusion.4 = f32[4,2,64]{2,1,0:T(2,128)S(1)} fusion(f32[4,2,64,4096]{3,2,1,0:T(8,128)S(1)} %get-tuple-element.13, f32[4,2,64]{2,1,0:T(2,128)S(1)} %get-tuple-element.12, pred[4,2,4096]{2,1,0:T(4,128)(4,1)S(1)} %broadcast_and_fusion), kind=kLoop, calls=%fused_computation.7 | loop fusion | flops 10485248 | bytes 8425472 | tf_op jit(solution)/shard_map/reduce_sum | solution.py:65
  51.8 0.7 copy.51
  52.5 5.6 %all-to-all-start.2 = ((f32[1,4,128]{1,0,2:T(1,128)}), f32[1,4,128]{1,0,2:T(1,128)S(1)}, u32[]{:S(2)}, u32[]{:S(2)}) async-start(f32[1,4,128]{1,0,2:T(1,128)} %bitcast.19), calls=%async_computation.2 | async-start | bytes 131072 | tf_op jit(solution)/shard_map/all_to_all | solution.py:76
  58.2 0.7 copy.42
  58.9 25.6 %copy.38 = bf16[1,4,4096,576]{3,2,1,0:T(8,128)(2,1)} copy(bf16[1,4,4096,576]{2,3,1,0:T(8,128)(2,1)} %param.8) | data formatting | bytes 37748736 | tf_op args[0]
  84.5 6.0 %all-to-all-start.1 = ((f32[1,4,128]{1,0,2:T(1,128)}), f32[1,4,128]{1,0,2:T(1,128)S(1)}, u32[]{:S(2)}, u32[]{:S(2)}) async-start(f32[1,4,128]{1,0,2:T(1,128)} %bitcast.15), calls=%async_computation.1 | async-start | bytes 131072 | tf_op jit(solution)/shard_map/all_to_all | solution.py:75
  90.6 9.9 %fusion.2 = f32[4,2,64,512]{3,2,1,0:T(8,128)S(1)} fusion(bf16[4,4096,576]{2,1,0:T(8,128)(2,1)} %bitcast.66, f32[4,2,64,4096]{3,2,1,0:T(8,128)} %copy-done.1, f32[4,2,64]{2,1,0:T(2,128)S(1)} %get-tuple-element.12, pred[4,2,4096]{2,1,0:T(4,128)(4,1)S(1)} %broadcast_and_fusion), kind=kOutput, calls=%fused_computation.3 | convolution fusion | flops 2157969408 | bytes 26249216 | tf_op jit(solution)/shard_map/bght,btv->bghv/dot_general | solution.py:66
  100.4 1.7 copy.40
  102.1 6.0 %all-to-all-start = ((f32[1,4,128,512]{3,1,0,2:T(4,128)}), f32[1,4,128,512]{3,1,0,2:T(4,128)S(1)}, u32[]{:S(2)}, u32[]{:S(2)}) async-start(f32[1,4,128,512]{3,1,0,2:T(4,128)} %copy.40), calls=%async_computation | async-start | bytes 2097152 | tf_op jit(solution)/shard_map/all_to_all | solution.py:79
  108.2 38.8 %all_gather.10 = bf16[1,4,64]{1,0,2:T(2,128)(2,1)S(1)} all-gather(bf16[1,4,8]{1,0,2:T(2,128)(2,1)S(1)} %copy.36), channel_id=1, replica_groups=mesh['groups'=2,'seq'=8,'section'=2] {'seq'}, dimensions={2}, use_global_device_ids=true | all-gather | bytes 576 | tf_op jit(solution)/shard_map/all_gather | solution.py:40
  147.1 26.0 %all_gather.9 = bf16[1,4,64,128]{3,2,1,0:T(8,128)(2,1)S(1)} all-gather(bf16[1,4,8,128]{3,2,1,0:T(8,128)(2,1)S(1)} %copy-done.2), channel_id=1, replica_groups=mesh['groups'=2,'seq'=8,'section'=2] {'seq'}, dimensions={2}, use_global_device_ids=true | all-gather | bytes 73728 | tf_op jit(solution)/shard_map/all_gather | solution.py:39
  173.1 3.8 %fusion.17 = f32[4,4096]{1,0:T(4,128)S(1)} fusion(f32[4,64]{1,0:T(4,128)S(1)} %copy.37, bf16[1,4,4096,128]{3,2,1,0:T(8,128)(2,1)} %param.9, bf16[1,4,64,128]{3,2,1,0:T(8,128)(2,1)S(1)} %all_gather.9), kind=kOutput, calls=%fused_computation.21 | convolution fusion | flops 272613376 | bytes 4326400 | tf_op jit(solution)/shard_map/bhd,btd->bht/dot_general | solution.py:47
  176.9 0.7 bitcast_select_fusion
  177.6 0.1 copy.45
  177.7 0.1 copy.43
  177.9 0.3 fusion.26
  178.4 0.4 fusion.23
  178.7 0.6 copy.47
  (20 shorter events, 0.4 us)
Async XLA Ops:
  0.6 177.7 %copy-start = (bf16[1,16,512,128]{3,2,1,0:T(8,128)(2,1)S(1)}, bf16[1,16,512,128]{3,2,1,0:T(8,128)(2,1)}, u32[]{:S(2)}) copy-start(bf16[1,16,512,128]{3,2,1,0:T(8,128)(2,1)} %param.13) | copy-start | bytes 6291460
  45.7 3.3 %copy-start.1 = (f32[4,2,64,4096]{3,2,1,0:T(8,128)}, f32[4,2,64,4096]{3,2,1,0:T(8,128)S(1)}, u32[]{:S(2)}) copy-start(f32[4,2,64,4096]{3,2,1,0:T(8,128)S(1)} %get-tuple-element.13) | copy-start | bytes 25165828
  52.5 32.0 %all-to-all-start.2 = ((f32[1,4,128]{1,0,2:T(1,128)}), f32[1,4,128]{1,0,2:T(1,128)S(1)}, u32[]{:S(2)}, u32[]{:S(2)}) async-start(f32[1,4,128]{1,0,2:T(1,128)} %bitcast.19), calls=%async_computation.2 | async-start | bytes 131072 | tf_op jit(solution)/shard_map/all_to_all | solution.py:76
  84.5 17.6 %all-to-all-start.1 = ((f32[1,4,128]{1,0,2:T(1,128)}), f32[1,4,128]{1,0,2:T(1,128)S(1)}, u32[]{:S(2)}, u32[]{:S(2)}) async-start(f32[1,4,128]{1,0,2:T(1,128)} %bitcast.15), calls=%async_computation.1 | async-start | bytes 131072 | tf_op jit(solution)/shard_map/all_to_all | solution.py:75
  90.5 17.6 %copy-start.4 = (bf16[1,4,8]{2,1,0:T(4,128)(2,1)S(1)}, bf16[1,4,8]{2,1,0:T(4,128)(2,1)}, u32[]{:S(2)}) copy-start(bf16[1,4,8]{2,1,0:T(4,128)(2,1)} %param.12) | copy-start | bytes 196
  90.6 56.6 %copy-start.2 = (bf16[1,4,8,128]{3,2,1,0:T(8,128)(2,1)S(1)}, bf16[1,4,8,128]{3,2,1,0:T(8,128)(2,1)}, u32[]{:S(2)}) copy-start(bf16[1,4,8,128]{3,2,1,0:T(8,128)(2,1)} %param.11) | copy-start | bytes 24580
  100.4 76.5 %copy-start.3 = (s32[4]{0:T(128)S(1)}, s32[4]{0:T(128)}, u32[]{:S(2)}) copy-start(s32[4]{0:T(128)} %param.15) | copy-start | bytes 52
  102.1 75.8 %all-to-all-start = ((f32[1,4,128,512]{3,1,0,2:T(4,128)}), f32[1,4,128,512]{3,1,0,2:T(4,128)S(1)}, u32[]{:S(2)}, u32[]{:S(2)}) async-start(f32[1,4,128,512]{3,1,0,2:T(4,128)} %copy.40), calls=%async_computation | async-start | bytes 2097152 | tf_op jit(solution)/shard_map/all_to_all | solution.py:79
where the time goes:
time: 180 us; the launch traced here: 179 us
  blocking collectives  98.5 us (55%)
  local copies, waits for them, and re-layouts  33.1 us (18%)
  matrix products  22.8 us (13%)
  starting transfers between devices  17.6 us (10%)
  other arithmetic  6.56 us (4%)
    all_gather x1, blocking collectives, on_device(): lax.all_gather(index_weight, 'seq', axis=2, tiled=True)  38.8 us
    all_gather x1, blocking collectives, on_device(): lax.all_gather(latent_query, 'seq', axis=2, tiled=True)  33.8 us
    unnamed x13, local copies, waits for them, and re-layouts  29.7 us
    all_gather x1, blocking collectives, on_device(): lax.all_gather(index_query, 'seq', axis=2, tiled=True)  26 us
    dot_general x1, matrix products, on_device(): jnp.einsum('bght,btv->bghv', soft_weights.astype(jnp.bfloat16), latent_st...  9.85 us
    dot_general x1, matrix products, on_device(): jnp.einsum('bghd,btd->bght', group_split, latent_state, preferred_element...  8.74 us
    all_to_all x1, starting transfers between devices, on_device(): lax.all_to_all(row_max[None], 'seq', split_axis=2, concat_axis=0, tiled=T...  6 us
    all_to_all x1, starting transfers between devices, on_device(): lax.all_to_all(partial_output[None], 'seq', split_axis=2, concat_axis=0,...  6 us
  transfers between devices with their start and end apart: 3, of which 0 were waited for; matrix products, arithmetic and copies ran while one was open for 24% of the time, Pallas kernels for 0%

commit v1 on v0

v1 whole, which is shorter than its diff:
```python
import functools

import jax
import jax.numpy as jnp
from jax import lax
from jax.experimental import pallas as pl
from jax.experimental.pallas import tpu as pltpu
from jax.sharding import PartitionSpec as P

LATENT_WIDTH = 512
ROTARY_WIDTH = 64
VALUE_WIDTH = 128
IDX_DIM = 128
BLOCK = 64
HEAD_GROUPS = 2
NEG = -1e30
CHUNK = 8
LANES = 128
MESH = pl.DeviceIdType.MESH


def greet_all(n, me):
    barrier = pltpu.get_barrier_semaphore()
    for k in range(1, n):
        pl.semaphore_signal(
            barrier, inc=1, device_id={"seq": lax.rem(me + k, n)}, device_id_type=MESH
        )
    pl.semaphore_wait(barrier, n - 1)


def push(n, me, k, src, dst, send_sem, recv_sem):
    return pltpu.make_async_remote_copy(
        src_ref=src,
        dst_ref=dst,
        send_sem=send_sem.at[k],
        recv_sem=recv_sem.at[k],
        device_id={"seq": lax.rem(me + k, n)},
        device_id_type=MESH,
    )


def gather_kernel(
    n, lens, lq, iqx, keys, gq, scores, giq, kbuf,
    key_sem, own_sem, isend, irecv, qsend, qrecv,
):
    me = lax.axis_index("seq")
    rows, span, _ = keys.shape
    loads = []
    for b in range(rows):
        copy = pltpu.make_async_copy(keys.at[b], kbuf.at[b], key_sem.at[b])
        copy.start()
        loads.append(copy)
    own = [
        pltpu.make_async_copy(iqx, giq.at[me], own_sem.at[0]),
        pltpu.make_async_copy(lq, gq.at[me], own_sem.at[1]),
    ]
    for copy in own:
        copy.start()
    greet_all(n, me)
    small = [push(n, me, k, iqx, giq.at[me], isend, irecv) for k in range(1, n)]
    large = [push(n, me, k, lq, gq.at[me], qsend, qrecv) for k in range(1, n)]
    for copy in small:
        copy.start()
    for copy in large:
        copy.start()
    for copy in loads:
        copy.wait()
    own[0].wait()
    for copy in small:
        copy.wait_recv()
    tile = min(512, span)
    lane = lax.broadcasted_iota(jnp.int32, (1, tile), 1)
    for b in range(rows):
        packed = giq[:, b].astype(jnp.float32)
        packed = packed.reshape(packed.shape[0] * packed.shape[1], packed.shape[2])
        query = packed[:, :IDX_DIM].astype(jnp.bfloat16)
        weight = packed[:, IDX_DIM:] * IDX_DIM ** (-0.5)
        length = lens[b]

        def step(c, carry, b=b, query=query, weight=weight, length=length):
            start = pl.multiple_of(c * tile, tile)
            dots = lax.dot_general(
                query,
                kbuf[b, pl.ds(start, tile), :],
                (((1,), (1,)), ((), ())),
                preferred_element_type=jnp.float32,
            )
            pieces = []
            for j in range(tile // 128):
                part = jnp.maximum(dots[:, j * 128 : (j + 1) * 128], 0.0) * weight
                pieces.append(jnp.sum(part, axis=0, keepdims=True))
            total = jnp.concatenate(pieces, axis=1)
            live = me * span + c * tile + lane < length
            scores[b : b + 1, pl.ds(start, tile)] = jnp.where(live, total, 0.0)
            return carry

        lax.fori_loop(0, span // tile, step, 0)
    own[1].wait()
    for copy in large:
        copy.wait_recv()
    for copy in small + large:
        copy.wait_send()


def local_kernel(sel, lens, gq, cache, parts, stats, buf, counts, low, high, sems):
    me = lax.axis_index("seq")
    rows, width, span = cache.shape
    nsel = sel.shape[2]
    here = span // BLOCK
    first = me * here

    def block_copy(b, rg, block, slot):
        start = pl.multiple_of((block - first) // 2 * LANES, LANES)
        dest = pl.multiple_of(slot * LANES, LANES)
        return pltpu.make_async_copy(
            cache.at[b, :, pl.ds(start, LANES)],
            buf.at[rg, :, pl.ds(dest, LANES)],
            sems.at[rg, slot],
        )

    for b in range(rows):
        for g in range(HEAD_GROUPS):
            rg = b * HEAD_GROUPS + g

            def scan(i, slot, b=b, g=g, rg=rg):
                block = sel[b, g, i]
                mine = jnp.logical_and(block >= first, block < first + here)

                @pl.when(mine)
                def _():
                    block_copy(b, rg, block, slot).start()
                    begin = block % 2 * BLOCK
                    low[rg, slot] = begin
                    high[rg, slot] = begin + jnp.minimum(BLOCK, lens[b] - block * BLOCK)

                return slot + mine.astype(jnp.int32)

            counts[rg] = lax.fori_loop(0, nsel, scan, jnp.int32(0), unroll=4)

    heads = gq.shape[2]
    per_group = gq.shape[0] // HEAD_GROUPS
    group_wise = per_group * heads
    tokens = CHUNK * LANES
    scale = (VALUE_WIDTH + ROTARY_WIDTH) ** (-0.5)
    lane = lax.broadcasted_iota(jnp.int32, (1, LANES), 1)
    for g in range(HEAD_GROUPS):
        table = jnp.zeros((group_wise, LANES), jnp.float32)
        for b in range(rows):
            rg = b * HEAD_GROUPS + g
            count = counts[rg]
            steps = jnp.maximum((count + CHUNK - 1) // CHUNK, 1)

            @pl.loop(count, steps * CHUNK)
            def _(slot, rg=rg):
                dest = pl.multiple_of(slot * LANES, LANES)
                buf[rg, :, pl.ds(dest, LANES)] = jnp.zeros((width, LANES), jnp.bfloat16)
                low[rg, slot] = 0
                high[rg, slot] = 0

            @pl.loop(0, count)
            def _(slot, b=b, rg=rg):
                block_copy(b, rg, first, slot).wait()

            query = gq[g * per_group : (g + 1) * per_group, b].reshape(group_wise, width)

            def chunk(c, rg=rg, query=query):
                base = pl.multiple_of(c * tokens, tokens)
                s = jnp.dot(
                    query,
                    buf[rg, :, pl.ds(base, tokens)],
                    preferred_element_type=jnp.float32,
                ) * scale
                bounds = [
                    (low[rg, c * CHUNK + j], high[rg, c * CHUNK + j]) for j in range(CHUNK)
                ]
                usable = jnp.concatenate(
                    [
                        ((lane >= lo) & (lane < hi)).astype(jnp.int32)
                        for lo, hi in bounds
                    ],
                    axis=1,
                ) > 0
                s = jnp.where(usable, s, NEG)
                return s, usable, buf[rg, :LATENT_WIDTH, pl.ds(base, tokens)]

            def mix(p, values):
                return lax.dot_general(
                    p.astype(jnp.bfloat16),
                    values,
                    (((1,), (1,)), ((), ())),
                    preferred_element_type=jnp.float32,
                )

            s, usable, values = chunk(0)
            top = jnp.max(s, axis=1, keepdims=True)
            p = jnp.where(usable, jnp.exp(s - top), 0.0)
            total = jnp.sum(p, axis=1, keepdims=True)
            acc = mix(p, values)

            def more(c, carry, chunk=chunk):
                top, total, acc = carry
                s, usable, values = chunk(c)
                new = jnp.maximum(top, jnp.max(s, axis=1, keepdims=True))
                p = jnp.where(usable, jnp.exp(s - new), 0.0)
                keep = jnp.exp(top - new)
                total = total * keep + jnp.sum(p, axis=1, keepdims=True)
                return new, total, acc * keep + mix(p, values)

            top, total, acc = lax.fori_loop(1, steps, more, (top, total, acc))
            parts[g * per_group : (g + 1) * per_group, b] = acc.astype(jnp.bfloat16).reshape(
                per_group, heads, LATENT_WIDTH
            )
            table = jnp.where(lane == 2 * b, top, table)
            table = jnp.where(lane == 2 * b + 1, total, table)
        stats[g * per_group : (g + 1) * per_group] = table.reshape(per_group, heads, LANES)


def exchange_kernel(
    n, parts, stats, weight, out, rparts, rstats, wbuf,
    own_sem, psend, precv, ssend, srecv,
):
    me = lax.axis_index("seq")
    _, rows, heads, latent = parts.shape
    own = [
        pltpu.make_async_copy(weight, wbuf, own_sem.at[0]),
        pltpu.make_async_copy(parts.at[me], rparts.at[me], own_sem.at[1]),
        pltpu.make_async_copy(stats.at[me], rstats.at[me], own_sem.at[2]),
    ]
    for copy in own:
        copy.start()
    greet_all(n, me)
    sends = []
    for k in range(1, n):
        peer = lax.rem(me + k, n)
        sends.append(push(n, me, k, stats.at[peer], rstats.at[me], ssend, srecv))
        sends.append(push(n, me, k, parts.at[peer], rparts.at[me], psend, precv))
    for copy in sends:
        copy.start()
    for copy in own:
        copy.wait()
    for copy in sends:
        copy.wait_recv()
    table = rstats[...]
    attended = []
    for b in range(rows):
        tops = [table[s, :, 2 * b : 2 * b + 1] for s in range(n)]
        joint = functools.reduce(jnp.maximum, tops)
        total = jnp.zeros_like(joint)
        acc = jnp.zeros((heads, latent), jnp.float32)
        for s in range(n):
            factor = jnp.exp(tops[s] - joint)
            total = total + factor * table[s, :, 2 * b + 1 : 2 * b + 2]
            acc = acc + factor * rparts[s, b].astype(jnp.float32)
        attended.append(acc / total)
    attended = jnp.concatenate(attended, axis=0).astype(jnp.bfloat16)
    which = lax.broadcasted_iota(jnp.int32, (rows * heads, 1), 0) % heads

    def project(h, acc):
        y = jnp.dot(attended, wbuf[h], preferred_element_type=jnp.float32)
        return jnp.where(which == h, y, acc)

    y = jnp.zeros((rows * heads, weight.shape[2]), jnp.float32)
    y = lax.fori_loop(0, heads, project, y, unroll=4)
    out[...] = y.reshape(rows, heads, weight.shape[2]).astype(out.dtype)
    for copy in sends:
        copy.wait_send()


def on_device(
    n,
    latent_cache,
    index_keys,
    latent_query,
    index_query,
    index_weight,
    value_up_weight,
    selected,
    lengths,
):
    cache, keys, lq = latent_cache[0], index_keys[0], latent_query[0]
    iq, iw, weight, sel = index_query[0], index_weight[0], value_up_weight[0], selected[0]
    rows, span, width = cache.shape
    heads = lq.shape[1]
    extra = -iq.shape[1] % 8
    iqx = jnp.concatenate(
        [iq, jnp.broadcast_to(iw[:, :, None], iw.shape + (128,))], axis=2
    )
    iqx = jnp.pad(iqx, ((0, 0), (0, extra), (0, 0)))
    vmem = pl.BlockSpec(memory_space=pltpu.VMEM)
    smem = pl.BlockSpec(memory_space=pltpu.SMEM)
    hbm = pl.BlockSpec(memory_space=pl.ANY)
    dma = pltpu.SemaphoreType.DMA
    limit = 60 * 1024 * 1024

    gq, index_scores = pl.pallas_call(
        functools.partial(gather_kernel, n),
        out_shape=(
            jax.ShapeDtypeStruct((n,) + lq.shape, lq.dtype),
            jax.ShapeDtypeStruct((rows, span), jnp.float32),
        ),
        in_specs=[smem, vmem, vmem, hbm],
        out_specs=(hbm, vmem),
        scratch_shapes=[
            pltpu.VMEM((n,) + iqx.shape, iqx.dtype),
            pltpu.VMEM(keys.shape, keys.dtype),
            dma((rows,)), dma((2,)), dma((n,)), dma((n,)), dma((n,)), dma((n,)),
        ],
        compiler_params=pltpu.CompilerParams(
            collective_id=0, has_side_effects=True, vmem_limit_bytes=limit
        ),
        name="gather",
    )(lengths, lq, iqx, keys)

    whole_heads = n * heads
    if heads % 16:
        gq = gq.transpose(1, 0, 2, 3).reshape(
            rows, HEAD_GROUPS, whole_heads // HEAD_GROUPS, width
        ).transpose(1, 0, 2, 3)
    slots = gq.shape[0]
    wide = gq.shape[2]
    pairs = rows * HEAD_GROUPS
    nsel = sel.shape[2]
    room = -(-nsel // CHUNK) * CHUNK
    parts, stats = pl.pallas_call(
        local_kernel,
        out_shape=(
            jax.ShapeDtypeStruct((slots, rows, wide, LATENT_WIDTH), jnp.bfloat16),
            jax.ShapeDtypeStruct((slots, wide, 128), jnp.float32),
        ),
        in_specs=[smem, smem, vmem, hbm],
        out_specs=(vmem, vmem),
        scratch_shapes=[
            pltpu.VMEM((pairs, width, room * LANES), cache.dtype),
            pltpu.SMEM((pairs,), jnp.int32),
            pltpu.SMEM((pairs, room), jnp.int32),
            pltpu.SMEM((pairs, room), jnp.int32),
            dma((pairs, nsel)),
        ],
        compiler_params=pltpu.CompilerParams(vmem_limit_bytes=limit),
        name="local",
    )(sel, lengths, gq, jnp.swapaxes(cache, 1, 2))
    if slots != n:
        parts = parts.transpose(1, 0, 2, 3).reshape(rows, n, heads, LATENT_WIDTH)
        parts = parts.transpose(1, 0, 2, 3)
        stats = stats.reshape(n, heads, 128)

    head_out = pl.pallas_call(
        functools.partial(exchange_kernel, n),
        out_shape=jax.ShapeDtypeStruct((rows, heads, weight.shape[2]), jnp.bfloat16),
        in_specs=[hbm, hbm, hbm],
        out_specs=vmem,
        scratch_shapes=[
            pltpu.VMEM(parts.shape, parts.dtype),
            pltpu.VMEM(stats.shape, stats.dtype),
            pltpu.VMEM(weight.shape, weight.dtype),
            dma((3,)), dma((n,)), dma((n,)), dma((n,)), dma((n,)),
        ],
        compiler_params=pltpu.CompilerParams(
            collective_id=1, has_side_effects=True, vmem_limit_bytes=limit
        ),
        name="exchange",
    )(parts, stats, weight)
    return (index_scores[None], head_out[None])


def solution(mesh):
    return jax.shard_map(
        functools.partial(on_device, mesh.shape["seq"]),
        mesh=mesh,
        in_specs=(
            P("section", "groups", "seq", None),
            P("section", "groups", "seq", None),
            P("section", "groups", "seq", None),
            P("section", "groups", "seq", None),
            P("section", "groups", "seq"),
            P("section", "seq", None, None),
            P("section", "groups", None, None),
            P("groups"),
        ),
        out_specs=(P("section", "groups", "seq"), P("section", "groups", "seq", None)),
        check_vma=False,
    )
```

time: 180 us -> 64.6 us (0.36)
  the two profiles are of different devices: /device:TPU:0 before, /device:TPU:14 now
where the time goes in v1:
time: 64.6 us; the launch traced here: 63.6 us
  Pallas kernels  58.9 us (91%)
  local copies, waits for them, and re-layouts  2.71 us (4%)
  other arithmetic  1.31 us (2%)
  between operations  0.67 us (1%)
    pallas_call x1, Pallas kernels, on_device(): pl.pallas_call(functools.partial(gather_kernel, n), out_shape=(jax.ShapeD...  23.4 us
    pallas_call x1, Pallas kernels, on_device(): pl.pallas_call(local_kernel, out_shape=(jax.ShapeDtypeStruct((slots, rows...  17.9 us
    pallas_call x1, Pallas kernels, on_device(): pl.pallas_call(functools.partial(exchange_kernel, n), out_shape=jax.Shape...  17.6 us
    unnamed x4, local copies, waits for them, and re-layouts  1.96 us
    concatenate x1, other arithmetic, on_device(): jnp.concatenate([iq, jnp.broadcast_to(iw[:, :, None], iw.shape + (128,))]...  1.31 us

profile of v1, /device:TPU:14, one launch (start us, length us, event | category | flops | bytes accessed | tf_op | source)
XLA Modules:
  0.0 63.6 jit_solution(17005879254379698979)
XLA Ops:
  0.6 0.8 %broadcast_in_dim.14 = bf16[4,8,128]{2,1,0:T(8,128)(2,1)S(1)} broadcast(bf16[4,8]{1,0:T(4,128)(2,1)} %bitcast.19), dimensions={0,1} | broadcast | bytes 8256 | tf_op jit(solution)/shard_map/broadcast_in_dim | solution.py:286
  1.4 1.3 %pad_maximum_fusion.iqx = bf16[4,8,256]{2,1,0:T(8,128)(2,1)} fusion(bf16[4,8,128]{2,1,0:T(8,128)(2,1)S(1)} %broadcast_in_dim.14, bf16[4,8,128]{2,1,0:T(8,128)(2,1)} %bitcast.17), kind=kLoop, calls=%fused_computation | loop fusion | flops 32768 | bytes 32768 | tf_op jit(solution)/shard_map/concatenate | solution.py:285
  2.7 23.4 %gather.1 = (bf16[8,4,16,576]{3,2,1,0:T(8,128)(2,1)}, f32[4,4096]{1,0:T(4,128)}) custom-call(s32[4]{0:T(128)} %lens.3, bf16[4,16,576]{2,1,0:T(8,128)(2,1)} %bitcast.14, bf16[4,8,256]{2,1,0:T(8,128)(2,1)} %pad_maximum_fusion.iqx, bf16[4,4096,128]{2,1,0:T(8,128)(2,1)} %bitcast.12), custom_call_target="tpu_custom_call" | custom-call | tf_op jit(solution)/shard_map/gather/pallas_call | solution.py:295
  26.1 0.0 copy-start
  26.1 17.9 %local.1 = (bf16[8,4,16,512]{3,2,1,0:T(8,128)(2,1)}, f32[8,16,128]{2,1,0:T(8,128)}) custom-call(s32[4,2,32]{2,1,0:T(2,128)} %bitcast.18, s32[4]{0:T(128)} %lens.3, bf16[8,4,16,576]{3,2,1,0:T(8,128)(2,1)} %get-tuple-element.7.gq, bf16[4,576,4096]{2,1,0:T(8,128)(2,1)} %bitcast.11), custom_call_target="tpu_custom_call" | custom-call | tf_op jit(solution)/shard_map/local/pallas_call | solution.py:324
  44.0 17.6 %exchange.1 = bf16[4,16,128]{2,1,0:T(8,128)(2,1)} custom-call(bf16[8,4,16,512]{3,2,1,0:T(8,128)(2,1)} %get-tuple-element.8.parts, f32[8,16,128]{2,1,0:T(8,128)} %get-tuple-element.9.stats, bf16[16,512,128]{2,1,0:T(8,128)(2,1)} %bitcast.13), custom_call_target="tpu_custom_call" | custom-call | tf_op jit(solution)/shard_map/exchange/pallas_call | solution.py:347
  61.6 0.0 copy-done
  61.6 0.6 copy.12
  62.2 1.3 %copy.13 = bf16[1,4,16,128]{3,2,1,0:T(8,128)(2,1)} copy(bf16[1,4,16,128]{3,2,1,0:T(8,128)(2,1)} %bitcast.15) | data formatting | bytes 32768
Async XLA Ops:
  26.1 35.5 %copy-start = (f32[4,4096]{1,0:T(4,128)S(1)}, f32[4,4096]{1,0:T(4,128)}, u32[]{:S(2)}) copy-start(f32[4,4096]{1,0:T(4,128)} %get-tuple-element.6) | copy-start | bytes 196612

commit v2 on v1

--- a/solution.py
+++ b/solution.py
@@ -40,41 +40,92 @@
 
 
 def gather_kernel(
-    n, lens, lq, iqx, keys, gq, scores, giq, kbuf,
-    key_sem, own_sem, isend, irecv, qsend, qrecv,
+    n, lens, lq, iq, iw, keys, gq, scores, giq, giw, kbuf,
+    key_sem, own_sem, isend, irecv, wsend, wrecv, qsend, qrecv,
 ):
     me = lax.axis_index("seq")
     rows, span, _ = keys.shape
+    half = n // 2
+    partner = me + 1 - 2 * lax.rem(me, 2)
+    order = sorted(range(1, half), key=lambda k: min(k, half - k))
     loads = []
     for b in range(rows):
         copy = pltpu.make_async_copy(keys.at[b], kbuf.at[b], key_sem.at[b])
         copy.start()
         loads.append(copy)
     own = [
-        pltpu.make_async_copy(iqx, giq.at[me], own_sem.at[0]),
-        pltpu.make_async_copy(lq, gq.at[me], own_sem.at[1]),
+        pltpu.make_async_copy(iq, giq.at[me], own_sem.at[0]),
+        pltpu.make_async_copy(iw, giw.at[me], own_sem.at[1]),
+        pltpu.make_async_copy(lq, gq.at[me], own_sem.at[2]),
     ]
     for copy in own:
         copy.start()
     greet_all(n, me)
-    small = [push(n, me, k, iqx, giq.at[me], isend, irecv) for k in range(1, n)]
-    large = [push(n, me, k, lq, gq.at[me], qsend, qrecv) for k in range(1, n)]
-    for copy in small:
-        copy.start()
-    for copy in large:
-        copy.start()
+
+    def push(peer, k, src, dst, send_sem, recv_sem):
+        return pltpu.make_async_remote_copy(
+            src_ref=src,
+            dst_ref=dst,
+            send_sem=send_sem.at[k],
+            recv_sem=recv_sem.at[k],
+            device_id={"seq": peer},
+            device_id_type=MESH,
+        )
+
+    def first_hop(src, dst, send_sem, recv_sem):
+        away = {
+            k: push(lax.rem(me + 2 * k, n), k, src, dst.at[me], send_sem, recv_sem)
+            for k in order
+        }
+        return away, push(partner, half, src, dst.at[me], send_sem, recv_sem)
+
+    def second_hop(dst, send_sem, recv_sem):
+        passed = {}
+        for k in order:
+            owner = lax.rem(me - 2 * k + n, n)
+            passed[k] = push(
+                partner, half + k, dst.at[owner], dst.at[owner], send_sem, recv_sem
+            )
+        return passed
+
+    small = [(iq, giq, isend, irecv), (iw, giw, wsend, wrecv)]
+    small_hops = [(first_hop(*x), second_hop(*x[1:])) for x in small]
+    (large, large_pair), large_on = first_hop(lq, gq, qsend, qrecv), second_hop(gq, qsend, qrecv)
+    for (away, pair), _ in small_hops:
+        for k in order:
+            away[k].start()
+        pair.start()
+    for k in order:
+        large[k].start()
+    large_pair.start()
+    for (away, _), passed in small_hops:
+        for k in order:
+            away[k].wait_recv()
+            passed[k].start()
     for copy in loads:
         copy.wait()
     own[0].wait()
-    for copy in small:
-        copy.wait_recv()
+    own[1].wait()
+    for (_, pair), passed in small_hops:
+        pair.wait_recv()
+        for k in order:
+            passed[k].wait_recv()
     tile = min(512, span)
     lane = lax.broadcasted_iota(jnp.int32, (1, tile), 1)
+    held = giq.shape[2]
+    given = iw.shape[1]
+    diagonal = (
+        lax.broadcasted_iota(jnp.int32, (n * held, given), 0) % held
+        == lax.broadcasted_iota(jnp.int32, (n * held, given), 1)
+    )
+    waiting = list(order)
     for b in range(rows):
-        packed = giq[:, b].astype(jnp.float32)
-        packed = packed.reshape(packed.shape[0] * packed.shape[1], packed.shape[2])
-        query = packed[:, :IDX_DIM].astype(jnp.bfloat16)
-        weight = packed[:, IDX_DIM:] * IDX_DIM ** (-0.5)
+        query = giq[:, b].astype(jnp.float32).reshape(n * held, giq.shape[3])
+        query = query.astype(jnp.bfloat16)
+        weight = giw[:, b : b + 1].astype(jnp.float32)
+        weight = jnp.broadcast_to(weight, (n, held, given)).reshape(n * held, given)
+        weight = jnp.sum(jnp.where(diagonal, weight, 0.0), axis=1, keepdims=True)
+        weight = jnp.broadcast_to(weight * IDX_DIM ** (-0.5), (n * held, LANES))
         length = lens[b]
 
         def step(c, carry, b=b, query=query, weight=weight, length=length):
@@ -86,8 +137,8 @@
                 preferred_element_type=jnp.float32,
             )
             pieces = []
-            for j in range(tile // 128):
-                part = jnp.maximum(dots[:, j * 128 : (j + 1) * 128], 0.0) * weight
+            for j in range(tile // LANES):
+                part = jnp.maximum(dots[:, j * LANES : (j + 1) * LANES], 0.0) * weight
                 pieces.append(jnp.sum(part, axis=0, keepdims=True))
             total = jnp.concatenate(pieces, axis=1)
             live = me * span + c * tile + lane < length
@@ -95,14 +146,25 @@
             return carry
 
         lax.fori_loop(0, span // tile, step, 0)
-    own[1].wait()
-    for copy in large:
-        copy.wait_recv()
-    for copy in small + large:
-        copy.wait_send()
-
-
-def local_kernel(sel, lens, gq, cache, parts, stats, buf, counts, low, high, sems):
+        if waiting:
+            k = waiting.pop(0)
+            large[k].wait_recv()
+            large_on[k].start()
+    for k in waiting:
+        large[k].wait_recv()
+        large_on[k].start()
+    own[2].wait()
+    large_pair.wait_recv()
+    for k in order:
+        large_on[k].wait_recv()
+    for (away, pair), passed in small_hops + [((large, large_pair), large_on)]:
+        pair.wait_send()
+        for k in order:
+            away[k].wait_send()
+            passed[k].wait_send()
+
+
+def local_kernel(sel, lens, gq, cache, parts, stats, buf, counts, kept, sems):
     me = lax.axis_index("seq")
     rows, width, span = cache.shape
     nsel = sel.shape[2]
@@ -124,18 +186,24 @@
 
             def scan(i, slot, b=b, g=g, rg=rg):
                 block = sel[b, g, i]
+                kept[rg, slot] = block
                 mine = jnp.logical_and(block >= first, block < first + here)
-
-                @pl.when(mine)
-                def _():
-                    block_copy(b, rg, block, slot).start()
-                    begin = block % 2 * BLOCK
-                    low[rg, slot] = begin
-                    high[rg, slot] = begin + jnp.minimum(BLOCK, lens[b] - block * BLOCK)
-
                 return slot + mine.astype(jnp.int32)
 
-            counts[rg] = lax.fori_loop(0, nsel, scan, jnp.int32(0), unroll=4)
+            count = lax.fori_loop(0, nsel, scan, jnp.int32(0), unroll=True)
+            counts[rg] = count
+
+            @pl.loop(0, count)
+            def _(slot, b=b, rg=rg):
+                block_copy(b, rg, kept[rg, slot], slot).start()
+
+    for rg in range(rows * HEAD_GROUPS):
+        count = counts[rg]
+
+        @pl.loop(count, jnp.maximum((count + CHUNK - 1) // CHUNK, 1) * CHUNK)
+        def _(slot, rg=rg):
+            dest = pl.multiple_of(slot * LANES, LANES)
+            buf[rg, :, pl.ds(dest, LANES)] = jnp.zeros((width, LANES), jnp.bfloat16)
 
     heads = gq.shape[2]
     per_group = gq.shape[0] // HEAD_GROUPS
@@ -150,29 +218,26 @@
             count = counts[rg]
             steps = jnp.maximum((count + CHUNK - 1) // CHUNK, 1)
 
-            @pl.loop(count, steps * CHUNK)
-            def _(slot, rg=rg):
-                dest = pl.multiple_of(slot * LANES, LANES)
-                buf[rg, :, pl.ds(dest, LANES)] = jnp.zeros((width, LANES), jnp.bfloat16)
-                low[rg, slot] = 0
-                high[rg, slot] = 0
-
             @pl.loop(0, count)
             def _(slot, b=b, rg=rg):
                 block_copy(b, rg, first, slot).wait()
 
             query = gq[g * per_group : (g + 1) * per_group, b].reshape(group_wise, width)
 
-            def chunk(c, rg=rg, query=query):
+            def chunk(c, b=b, rg=rg, query=query, count=count):
                 base = pl.multiple_of(c * tokens, tokens)
                 s = jnp.dot(
                     query,
                     buf[rg, :, pl.ds(base, tokens)],
                     preferred_element_type=jnp.float32,
                 ) * scale
-                bounds = [
-                    (low[rg, c * CHUNK + j], high[rg, c * CHUNK + j]) for j in range(CHUNK)
-                ]
+                bounds = []
+                for j in range(CHUNK):
+                    slot = c * CHUNK + j
+                    block = kept[rg, slot]
+                    begin = block % 2 * BLOCK
+                    live = jnp.minimum(BLOCK, lens[b] - block * BLOCK)
+                    bounds.append((begin, jnp.where(slot < count, begin + live, 0)))
                 usable = jnp.concatenate(
                     [
                         ((lane >= lo) & (lane < hi)).astype(jnp.int32)
@@ -282,10 +347,8 @@
     rows, span, width = cache.shape
     heads = lq.shape[1]
     extra = -iq.shape[1] % 8
-    iqx = jnp.concatenate(
-        [iq, jnp.broadcast_to(iw[:, :, None], iw.shape + (128,))], axis=2
-    )
-    iqx = jnp.pad(iqx, ((0, 0), (0, extra), (0, 0)))
+    if extra:
+        iq = jnp.pad(iq, ((0, 0), (0, extra), (0, 0)))
     vmem = pl.BlockSpec(memory_space=pltpu.VMEM)
     smem = pl.BlockSpec(memory_space=pltpu.SMEM)
     hbm = pl.BlockSpec(memory_space=pl.ANY)
@@ -298,18 +361,20 @@
             jax.ShapeDtypeStruct((n,) + lq.shape, lq.dtype),
             jax.ShapeDtypeStruct((rows, span), jnp.float32),
         ),
-        in_specs=[smem, vmem, vmem, hbm],
+        in_specs=[smem, vmem, vmem, vmem, hbm],
         out_specs=(hbm, vmem),
         scratch_shapes=[
-            pltpu.VMEM((n,) + iqx.shape, iqx.dtype),
+            pltpu.VMEM((n,) + iq.shape, iq.dtype),
+            pltpu.VMEM((n,) + iw.shape, iw.dtype),
             pltpu.VMEM(keys.shape, keys.dtype),
-            dma((rows,)), dma((2,)), dma((n,)), dma((n,)), dma((n,)), dma((n,)),
+            dma((rows,)), dma((3,)), dma((n,)), dma((n,)), dma((n,)), dma((n,)),
+            dma((n,)), dma((n,)),
         ],
         compiler_params=pltpu.CompilerParams(
             collective_id=0, has_side_effects=True, vmem_limit_bytes=limit
         ),
         name="gather",
-    )(lengths, lq, iqx, keys)
+    )(lengths, lq, iq, iw, keys)
 
     whole_heads = n * heads
     if heads % 16:
@@ -333,7 +398,6 @@
             pltpu.VMEM((pairs, width, room * LANES), cache.dtype),
             pltpu.SMEM((pairs,), jnp.int32),
             pltpu.SMEM((pairs, room), jnp.int32),
-            pltpu.SMEM((pairs, room), jnp.int32),
             dma((pairs, nsel)),
         ],
         compiler_params=pltpu.CompilerParams(vmem_limit_bytes=limit),

time: 64.6 us -> 56.7 us (0.88); the launches traced: 63.6 us -> 56.9 us
  Pallas kernels: 58.9 us -> 54.3 us
  other arithmetic: 1.31 us -> 0 us
  local copies, waits for them, and re-layouts: 2.71 us -> 1.96 us
    pallas_call x1, Pallas kernels: 23.4 us -> 19.4 us  [on_device(): pl.pallas_call(functools.partial(gather_kernel, n), out_shape=(jax.ShapeD...]
    pallas_call x1, Pallas kernels: 17.9 us -> 14.5 us  [on_device(): pl.pallas_call(local_kernel, out_shape=(jax.ShapeDtypeStruct((slots, rows...]
    pallas_call x1, Pallas kernels: 17.6 us -> 20.4 us  [on_device(): pl.pallas_call(functools.partial(exchange_kernel, n), out_shape=jax.Shape...]
    concatenate x1 -> x0, other arithmetic: 1.31 us -> none  [on_device(): jnp.concatenate([iq, jnp.broadcast_to(iw[:, :, None], iw.shape + (128,))]...]
    broadcast_in_dim x1 -> x0, local copies, waits for them, and re-layouts: 0.75 us -> none  [on_device(): jnp.broadcast_to(iw[:, :, None], iw.shape + (128,))]
where the time goes in v2:
time: 56.7 us; the launch traced here: 56.9 us
  Pallas kernels  54.3 us (96%)
  local copies, waits for them, and re-layouts  1.96 us (3%)
  between operations  0.67 us (1%)
    pallas_call x1, Pallas kernels, on_device(): pl.pallas_call(functools.partial(exchange_kernel, n), out_shape=jax.Shape...  20.4 us
    pallas_call x1, Pallas kernels, on_device(): pl.pallas_call(functools.partial(gather_kernel, n), out_shape=(jax.ShapeD...  19.4 us
    pallas_call x1, Pallas kernels, on_device(): pl.pallas_call(local_kernel, out_shape=(jax.ShapeDtypeStruct((slots, rows...  14.5 us
    unnamed x4, local copies, waits for them, and re-layouts  1.96 us

profile of v2, /device:TPU:14, one launch (start us, length us, event | category | flops | bytes accessed | tf_op | source)
XLA Modules:
  0.0 56.9 jit_solution(13134949781711768697)
XLA Ops:
  0.6 19.4 %gather.1 = (bf16[8,4,16,576]{3,2,1,0:T(8,128)(2,1)}, f32[4,4096]{1,0:T(4,128)}) custom-call(s32[4]{0:T(128)} %lens.3, bf16[4,16,576]{2,1,0:T(8,128)(2,1)} %bitcast.14, bf16[4,8,128]{2,1,0:T(8,128)(2,1)} %bitcast.17, bf16[4,8]{1,0:T(4,128)(2,1)} %bitcast.19, bf16[4,4096,128]{2,1,0:T(8,128)(2,1)} %bitcast.12), custom_call_target="tpu_custom_call" | custom-call | tf_op jit(solution)/shard_map/gather/pallas_call | solution.py:358
  20.1 0.0 copy-start
  20.1 14.5 %local.1 = (bf16[8,4,16,512]{3,2,1,0:T(8,128)(2,1)}, f32[8,16,128]{2,1,0:T(8,128)}) custom-call(s32[4,2,32]{2,1,0:T(2,128)} %bitcast.18, s32[4]{0:T(128)} %lens.3, bf16[8,4,16,576]{3,2,1,0:T(8,128)(2,1)} %get-tuple-element.7.gq, bf16[4,576,4096]{2,1,0:T(8,128)(2,1)} %bitcast.11), custom_call_target="tpu_custom_call" | custom-call | tf_op jit(solution)/shard_map/local/pallas_call | solution.py:389
  34.5 20.4 %exchange.1 = bf16[4,16,128]{2,1,0:T(8,128)(2,1)} custom-call(bf16[8,4,16,512]{3,2,1,0:T(8,128)(2,1)} %get-tuple-element.8.parts, f32[8,16,128]{2,1,0:T(8,128)} %get-tuple-element.9.stats, bf16[16,512,128]{2,1,0:T(8,128)(2,1)} %bitcast.13), custom_call_target="tpu_custom_call" | custom-call | tf_op jit(solution)/shard_map/exchange/pallas_call | solution.py:411
  55.0 0.0 copy-done
  55.0 0.6 %copy.12 = f32[1,4,4096]{2,1,0:T(4,128)} copy(f32[1,4,4096]{2,1,0:T(4,128)S(1)} %bitcast.16) | data formatting | bytes 131072
  55.6 1.3 %copy.13 = bf16[1,4,16,128]{3,2,1,0:T(8,128)(2,1)} copy(bf16[1,4,16,128]{3,2,1,0:T(8,128)(2,1)} %bitcast.15) | data formatting | bytes 32768
Async XLA Ops:
  20.1 34.9 %copy-start = (f32[4,4096]{1,0:T(4,128)S(1)}, f32[4,4096]{1,0:T(4,128)}, u32[]{:S(2)}) copy-start(f32[4,4096]{1,0:T(4,128)} %get-tuple-element.6) | copy-start | bytes 196612

commit v3 on v2

--- a/solution.py
+++ b/solution.py
@@ -88,28 +88,23 @@
             )
         return passed
 
-    small = [(iq, giq, isend, irecv), (iw, giw, wsend, wrecv)]
-    small_hops = [(first_hop(*x), second_hop(*x[1:])) for x in small]
+    small = []
+    for k in range(1, n):
+        peer = lax.rem(me + k, n)
+        small.append(push(peer, k, iq, giq.at[me], isend, irecv))
+        small.append(push(peer, k, iw, giw.at[me], wsend, wrecv))
     (large, large_pair), large_on = first_hop(lq, gq, qsend, qrecv), second_hop(gq, qsend, qrecv)
-    for (away, pair), _ in small_hops:
-        for k in order:
-            away[k].start()
-        pair.start()
+    for copy in small:
+        copy.start()
     for k in order:
         large[k].start()
     large_pair.start()
-    for (away, _), passed in small_hops:
-        for k in order:
-            away[k].wait_recv()
-            passed[k].start()
     for copy in loads:
         copy.wait()
     own[0].wait()
     own[1].wait()
-    for (_, pair), passed in small_hops:
-        pair.wait_recv()
-        for k in order:
-            passed[k].wait_recv()
+    for copy in small:
+        copy.wait_recv()
     tile = min(512, span)
     lane = lax.broadcasted_iota(jnp.int32, (1, tile), 1)
     held = giq.shape[2]
@@ -157,11 +152,12 @@
     large_pair.wait_recv()
     for k in order:
         large_on[k].wait_recv()
-    for (away, pair), passed in small_hops + [((large, large_pair), large_on)]:
-        pair.wait_send()
-        for k in order:
-            away[k].wait_send()
-            passed[k].wait_send()
+    for copy in small:
+        copy.wait_send()
+    large_pair.wait_send()
+    for k in order:
+        large[k].wait_send()
+        large_on[k].wait_send()
 
 
 def local_kernel(sel, lens, gq, cache, parts, stats, buf, counts, kept, sems):
@@ -410,7 +406,7 @@
 
     head_out = pl.pallas_call(
         functools.partial(exchange_kernel, n),
-        out_shape=jax.ShapeDtypeStruct((rows, heads, weight.shape[2]), jnp.bfloat16),
+        out_shape=jax.ShapeDtypeStruct((rows, heads, weight.shape[2]), jnp.float32),
         in_specs=[hbm, hbm, hbm],
         out_specs=vmem,
         scratch_shapes=[
@@ -424,7 +420,7 @@
         ),
         name="exchange",
     )(parts, stats, weight)
-    return (index_scores[None], head_out[None])
+    return (index_scores[None], head_out.astype(jnp.bfloat16)[None])
 
 
 def solution(mesh):

time: 56.7 us -> 54.5 us (0.961); the launches traced: 56.9 us -> 54 us
  Pallas kernels: 54.3 us -> 51.4 us
  other arithmetic: 0 us -> 1.37 us
  local copies, waits for them, and re-layouts: 1.96 us -> 0.63 us
    broadcast_in_dim x0 -> x1, other arithmetic: none -> 1.37 us  [on_device(): return (index_scores[None], head_out.astype(jnp.bfloat16)[None])]
    pallas_call x1, Pallas kernels: 20.4 us -> 19.1 us  [on_device(): pl.pallas_call(functools.partial(exchange_kernel, n), out_shape=jax.Shape...]
    unnamed x4 -> x3, local copies, waits for them, and re-layouts: 1.96 us -> 0.63 us
    pallas_call x1, Pallas kernels: 14.5 us -> 13.4 us  [on_device(): pl.pallas_call(local_kernel, out_shape=(jax.ShapeDtypeStruct((slots, rows...]
    pallas_call x1, Pallas kernels: 19.4 us -> 18.8 us  [on_device(): pl.pallas_call(functools.partial(gather_kernel, n), out_shape=(jax.ShapeD...]
where the time goes in v3:
time: 54.5 us; the launch traced here: 54 us
  Pallas kernels  51.4 us (94%)
  other arithmetic  1.37 us (3%)
  between operations  0.66 us (1%)
  local copies, waits for them, and re-layouts  0.63 us (1%)
    pallas_call x1, Pallas kernels, on_device(): pl.pallas_call(functools.partial(exchange_kernel, n), out_shape=jax.Shape...  19.1 us
    pallas_call x1, Pallas kernels, on_device(): pl.pallas_call(functools.partial(gather_kernel, n), out_shape=(jax.ShapeD...  18.8 us
    pallas_call x1, Pallas kernels, on_device(): pl.pallas_call(local_kernel, out_shape=(jax.ShapeDtypeStruct((slots, rows...  13.4 us
    broadcast_in_dim x1, other arithmetic, on_device(): return (index_scores[None], head_out.astype(jnp.bfloat16)[None])  1.37 us

profile of v3, /device:TPU:14, one launch (start us, length us, event | category | flops | bytes accessed | tf_op | source)
XLA Modules:
  0.0 54.0 jit_solution(14073561058366724819)
XLA Ops:
  0.6 18.8 %gather.1 = (bf16[8,4,16,576]{3,2,1,0:T(8,128)(2,1)}, f32[4,4096]{1,0:T(4,128)}) custom-call(s32[4]{0:T(128)} %lens.3, bf16[4,16,576]{2,1,0:T(8,128)(2,1)} %bitcast.15, bf16[4,8,128]{2,1,0:T(8,128)(2,1)} %bitcast.17, bf16[4,8]{1,0:T(4,128)(2,1)} %bitcast.19, bf16[4,4096,128]{2,1,0:T(8,128)(2,1)} %bitcast.13), custom_call_target="tpu_custom_call" | custom-call | tf_op jit(solution)/shard_map/gather/pallas_call | solution.py:354
  19.5 0.0 copy-start
  19.5 13.4 %local.1 = (bf16[8,4,16,512]{3,2,1,0:T(8,128)(2,1)}, f32[8,16,128]{2,1,0:T(8,128)}) custom-call(s32[4,2,32]{2,1,0:T(2,128)} %bitcast.18, s32[4]{0:T(128)} %lens.3, bf16[8,4,16,576]{3,2,1,0:T(8,128)(2,1)} %get-tuple-element.7.gq, bf16[4,576,4096]{2,1,0:T(8,128)(2,1)} %bitcast.12), custom_call_target="tpu_custom_call" | custom-call | tf_op jit(solution)/shard_map/local/pallas_call | solution.py:385
  32.9 19.1 %exchange.1 = f32[4,16,128]{2,1,0:T(8,128)} custom-call(bf16[8,4,16,512]{3,2,1,0:T(8,128)(2,1)} %get-tuple-element.8.parts, f32[8,16,128]{2,1,0:T(8,128)} %get-tuple-element.9.stats, bf16[16,512,128]{2,1,0:T(8,128)(2,1)} %bitcast.14), custom_call_target="tpu_custom_call" | custom-call | tf_op jit(solution)/shard_map/exchange/pallas_call | solution.py:407
  52.0 1.4 %convert_bitcast_fusion = bf16[1,4,16,128]{3,2,1,0:T(8,128)(2,1)} fusion(f32[4,16,128]{2,1,0:T(8,128)} %exchange.1), kind=kLoop, calls=%fused_computation | loop fusion | flops 8192 | bytes 49152 | tf_op jit(solution)/shard_map/broadcast_in_dim | solution.py:423
  53.4 0.0 copy-done
  53.4 0.6 %copy.11 = f32[1,4,4096]{2,1,0:T(4,128)} copy(f32[1,4,4096]{2,1,0:T(4,128)S(1)} %bitcast.16) | data formatting | bytes 131072
Async XLA Ops:
  19.5 33.9 %copy-start = (f32[4,4096]{1,0:T(4,128)S(1)}, f32[4,4096]{1,0:T(4,128)}, u32[]{:S(2)}) copy-start(f32[4,4096]{1,0:T(4,128)} %get-tuple-element.6) | copy-start | bytes 196612
